TPU v7x, 512 devices: a whole 4x8x8 slice. The times are simulated.
512 devices in a mesh: fsdp: 128 (over y, z, core), dp: 4 (over x).
Axes of the slice: x: 4, y: 8, z: 8, core: 2. Of those that a mesh axis runs over, the one named last changes fastest.
Arguments:
- tokens: bfloat16 [512, 4096], P('dp', 'fsdp'), may hold values from -6 to 6
- out_grad: bfloat16 [512, 5120], P('dp', 'fsdp'), may hold values from -0.26367188 to 0.26367188
- master: float32 [4096, 5120], P('fsdp'), may hold values from -0.09375 to 0.09375
- moment_one: float32 [4096, 5120], P('fsdp'), may hold values from -3 to 3
- moment_two: float32 [4096, 5120], P('fsdp'), may hold values from 0.1 to 4
- flags: int32 [512, 16], P(('fsdp', 'dp')), may hold values 0 or 1
- steps: int32 [16], replicated, may hold values from 1 to 8
- rate: float32 [1], replicated, may hold values from 0.001 to 0.01
Outputs:
- master_next: float32 [4096, 5120], P('fsdp')
- moment_one_next: float32 [4096, 5120], P('fsdp')
- moment_two_next: float32 [4096, 5120], P('fsdp')
- weight_half: bfloat16 [4096, 5120], P('fsdp')
- steps_next: int32 [16], replicated
- outputs: bfloat16 [512, 5120], P('dp', 'fsdp')
All inputs are finite; a program needn't handle non-finite values. No bound on the sum of `flags` on one device may be relied on, other than what follows from the above.
Results may differ from a plain program's by a relative error of at most 0.0049.
Values may be sent and summed in bfloat16 or wider, within the bound.
No kernel may reach another device: no remote copies, remote signals or barrier semaphores. Data moves between devices by JAX's collectives and lax.ppermute only.
A program may use at most 64 MiB of HBM per device.

v0:
```python
import jax
import jax.numpy as jnp
from jax import lax
from jax.sharding import Mesh
from jax.sharding import PartitionSpec as P

BUCKETS = 16
FSDP = ("fsdp_0", "fsdp_1", "fsdp_2")
FSDP_DP = ("fsdp_0", "fsdp_1", "fsdp_2", "dp")
first_decay = 0.9
second_decay = 0.95
epsilon = 1e-08


def joined_along(blocks, dim):
    blocks = jnp.moveaxis(blocks, 0, dim)
    shape = blocks.shape
    return blocks.reshape(*shape[:dim], shape[dim] * shape[dim + 1], *shape[dim + 2 :])


def all_blocks(x, axes, order):
    blocks = x[None]
    for k in order:
        blocks = lax.all_gather(blocks, axes[k], axis=0, tiled=True)
    current = [lax.axis_size(axes[k]) for k in reversed(order)]
    blocks = blocks.reshape(*current, *x.shape)
    turned = sorted(range(len(order)), key=lambda place: order[len(order) - 1 - place])
    return blocks.transpose(*turned, *range(len(order), blocks.ndim)).reshape(-1, *x.shape)


def gather_axes(x, axes, order, dim):
    return joined_along(all_blocks(x, axes, order), dim)


def over_axes(x, axes):
    for axis in axes:
        x = lax.psum(x, axis)
    return x


def from_everyone(x, axis):
    size = lax.axis_size(axis)
    return lax.all_to_all(jnp.broadcast_to(x[None], (size, *x.shape)), axis, 0, 0, tiled=True)


def of_everyone(x, axis):
    everything = from_everyone(x, axis)
    return jnp.sum(everything, axis=0)


def local(tokens, out_grad, master, moment_one, moment_two, flags, steps, rate):
    width_out = master.shape[1]
    bucket_width = width_out // BUCKETS
    contract_rows = (((0,), (0,)), ((), ()))
    partial_value = lax.dot_general(
        tokens,
        gather_axes(out_grad, (("fsdp_0", "fsdp_1"), "fsdp_2"), (0, 1), 1),
        contract_rows,
        preferred_element_type=jnp.float32,
    )
    counts = over_axes(flags[0], FSDP_DP)
    gradient = of_everyone(partial_value, "dp")
    commit_bucket = counts == 0
    commit = jnp.repeat(commit_bucket, bucket_width)[None, :]
    times = jnp.repeat(steps + 1, bucket_width).astype(jnp.float32)[None, :]
    first = first_decay * moment_one + (1.0 - first_decay) * gradient
    second = second_decay * moment_two + (1.0 - second_decay) * gradient * gradient
    fix_one = 1.0 - jnp.power(jnp.float32(first_decay), times)
    fix_two = 1.0 - jnp.power(jnp.float32(second_decay), times)
    candidate = master - rate[0] * (first / fix_one) / (jnp.sqrt(second / fix_two) + epsilon)
    master_next = jnp.where(commit, candidate, master)
    moment_one_next = jnp.where(commit, first, moment_one)
    moment_two_next = jnp.where(commit, second, moment_two)
    weight_half = master_next.astype(jnp.bfloat16)
    steps_next = steps + commit_bucket.astype(jnp.int32)
    weight_cols = lax.all_to_all(weight_half, FSDP, split_axis=1, concat_axis=0, tiled=True)
    result = jnp.dot(
        lax.all_gather(tokens, FSDP, axis=1, tiled=True),
        weight_cols,
        preferred_element_type=jnp.float32,
    )
    return (
        master_next,
        moment_one_next,
        moment_two_next,
        weight_half,
        steps_next,
        result.astype(jnp.bfloat16),
    )


def solution(mesh):
    split = Mesh(
        mesh.devices.reshape(8, 8, 2, mesh.shape["dp"]), ("fsdp_0", "fsdp_1", "fsdp_2", "dp")
    )
    in_specs = (
        P("dp", FSDP),
        P("dp", FSDP),
        P(FSDP, None),
        P(FSDP, None),
        P(FSDP, None),
        P(FSDP_DP, None),
        P(),
        P(),
    )
    out_specs = (P(FSDP, None), P(FSDP, None), P(FSDP, None), P(FSDP, None), P(), P("dp", FSDP))
    return jax.shard_map(local, mesh=split, in_specs=in_specs, out_specs=out_specs, check_vma=False)
```

profile of v0, /device:TPU:1, one launch (start us, length us, event | category | flops | bytes accessed | tf_op | source)
XLA Modules:
  0.0 188.4 jit_solution(5304647750274123168)
XLA Ops:
  8.0 0.0 all-gather.4.cloned.1.call-start
  8.0 47.0 %all-gather = bf16[8192,40]{0,1:T(8,128)(2,1)S(1)} all-gather(bf16[128,40]{0,1:T(8,128)(2,1)} %param.9), channel_id=2, replica_groups=mesh['fsdp_0'=8,'fsdp_1'=8,'fsdp_2'=2,'dp'=4] {'fsdp_0','fsdp_1'}, dimensions={0}, use_global_device_ids=true | all-gather | bytes 665600 | tf_op jit(solution)/shard_map/all_gather | solution.py:24
  55.1 1.0 copy.30
  56.1 0.0 all-gather.4.cloned.1.call-update
  56.1 26.5 %all-gather.4.cloned.1.call-done = bf16[128,128,40]{1,0,2:T(8,128)(2,1)} async-done(((bf16[64,128,40]{1,0,2:T(8,128)(2,1)}), bf16[128,128,40]{1,0,2:T(8,128)(2,1)}) %all-gather.4.cloned.1.call-update) | async-done | bytes 1310736 | tf_op jit(solution)/shard_map/all_gather | solution.py:24
  82.6 2.2 %copy.25 = bf16[64,2,128,40]{2,3,1,0:T(8,128)(2,1)S(1)} copy(bf16[64,2,128,40]{2,0,1,3:T(8,128)(2,1)} %bitcast.33) | data formatting | bytes 2621440 | tf_op jit(solution)/shard_map/transpose | solution.py:28
  84.8 0.5 fusion.5
  85.3 1.8 broadcast_in_dim.38
  87.1 3.8 %all-to-all-start = ((f32[4,32,5120]{2,1,0:T(8,128)}), f32[4,32,5120]{2,1,0:T(8,128)S(1)}, u32[]{:S(2)}, u32[]{:S(2)}) async-start(f32[4,32,5120]{2,1,0:T(8,128)} %broadcast_in_dim.38), calls=%async_computation | async-start | bytes 5242880 | tf_op jit(solution)/shard_map/all_to_all | solution.py:43
  90.9 0.0 all-gather.6.cloned.1.call-start
  91.0 0.5 all-gather.6.cloned.1.call-update
  91.5 0.1 broadcast_in_dim.40
  91.6 0.1 sub.30
  91.7 0.1 broadcast_in_dim.39
  91.7 0.1 sub.28
  92.5 10.5 %psum.28 = s32[16]{0:T(128)S(1)} all-reduce(s32[16]{0:T(128)S(1)} %bitcast.34), channel_id=1, replica_groups=mesh['fsdp_0'=8,'fsdp_1'=8,'fsdp_2'=2,'dp'=4] {'fsdp_0'}, use_global_device_ids=true, to_apply=%region_0.0 | all-reduce | flops 16 | bytes 128 | tf_op jit(solution)/shard_map/psum | solution.py:37
  103.0 12.2 %psum.29 = s32[16]{0:T(128)S(1)} all-reduce(s32[16]{0:T(128)S(1)} %psum.28), channel_id=1, replica_groups=mesh['fsdp_0'=8,'fsdp_1'=8,'fsdp_2'=2,'dp'=4] {'fsdp_1'}, use_global_device_ids=true, to_apply=%region_1.0 | all-reduce | flops 16 | bytes 128 | tf_op jit(solution)/shard_map/psum | solution.py:37
  115.2 6.6 %psum.30 = s32[16]{0:T(128)S(1)} all-reduce(s32[16]{0:T(128)S(1)} %psum.29), channel_id=1, replica_groups=mesh['fsdp_0'=8,'fsdp_1'=8,'fsdp_2'=2,'dp'=4] {'fsdp_2'}, use_global_device_ids=true, to_apply=%region_2.0 | all-reduce | flops 16 | bytes 128 | tf_op jit(solution)/shard_map/psum | solution.py:37
  121.8 7.3 %psum.31 = s32[16]{0:T(128)S(1)} all-reduce(s32[16]{0:T(128)S(1)} %psum.30), channel_id=1, replica_groups=mesh['fsdp_0'=8,'fsdp_1'=8,'fsdp_2'=2,'dp'=4] {'dp'}, use_global_device_ids=true, to_apply=%region_3.0 | all-reduce | flops 16 | bytes 128 | tf_op jit(solution)/shard_map/psum | solution.py:37
  129.1 0.1 broadcast_in_dim.34
  129.2 0.1 broadcast_in_dim.35
  129.3 0.2 reduce_sum.9
  129.5 3.1 %fusion.4 = (bf16[32,5120]{1,0:T(8,128)(2,1)S(1)}, f32[32,5120]{1,0:T(8,128)}, f32[32,5120]{1,0:T(8,128)}, f32[32,5120]{1,0:T(8,128)}) fusion(f32[32,5120]{1,0:T(8,128)} %param.10, f32[5120]{0:T(1024)S(1)} %sub.30, f32[32,5120]{1,0:T(8,128)S(1)} %reduce_sum.9, f32[32,5120]{1,0:T(8,128)} %param.12, f32[5120]{0:T(1024)S(1)} %sub.28, f32[32,5120]{1,0:T(8,128)} %param.11, ...), kind=kLoop, calls=%fused_computation.12 | loop fusion | flops 2785280 | bytes 4961284 | tf_op jit(solution)/shard_map/convert_element_type | solution.py:74
  132.6 1.9 all_to_all.18
  134.5 0.7 copy.32
  135.2 2.4 %reshape.56 = bf16[128,2,640]{2,1,0:T(2,128)(2,1)} reshape(bf16[128,32,40]{2,1,0:T(8,128)(2,1)S(1)} %bitcast.30) | data formatting | bytes 655360
  137.6 10.5 %all-to-all-start.1 = ((bf16[128,2,640]{2,1,0:T(2,128)(2,1)}), bf16[128,2,640]{2,1,0:T(2,128)(2,1)S(1)}, u32[]{:S(2)}, u32[]{:S(2)}) async-start(bf16[128,2,640]{2,1,0:T(2,128)(2,1)} %reshape.56), calls=%async_computation.1 | async-start | bytes 655360 | tf_op jit(solution)/shard_map/all_to_all | solution.py:76
  148.0 0.5 convert_add_fusion
  148.6 15.3 %all-to-all-done.1 = bf16[128,2,640]{2,1,0:T(2,128)(2,1)S(1)} async-done(((bf16[128,2,640]{2,1,0:T(2,128)(2,1)}), bf16[128,2,640]{2,1,0:T(2,128)(2,1)S(1)}, u32[]{:S(2)}, u32[]{:S(2)}) %all-to-all-start.1) | async-done | bytes 327712 | tf_op jit(solution)/shard_map/all_to_all | solution.py:76
  163.9 1.6 reshape.57
  165.5 13.2 %all-gather.6.cloned.1.call-done = bf16[128,4096]{0,1:T(8,128)(2,1)} async-done(((bf16[128,32]{0,1:T(8,128)(2,1)}), bf16[128,4096]{0,1:T(8,128)(2,1)}) %all-gather.6.cloned.1.call-update) | async-done | bytes 1048592 | tf_op jit(solution)/shard_map/all_gather | solution.py:78
  178.7 2.3 %fusion = bf16[128,40]{0,1:T(8,128)(2,1)} fusion(bf16[4096,40]{1,0:T(8,128)(2,1)S(1)} %bitcast.29, bf16[128,4096]{0,1:T(8,128)(2,1)} %all-gather.6.cloned.1.call-done), kind=kOutput, calls=%fused_computation.1 | convolution fusion | flops 41948160 | bytes 1386496 | tf_op jit(solution)/shard_map/dot_general | solution.py:77
  (11 shorter events, 0.0 us)
Async XLA Ops:
  8.0 74.6 %all-gather.4.cloned.1.call-start = ((), (), s32[]{:S(2)}) async-start(), calls=%async_computation.2 | async-start | bytes 1966080 | tf_op jit(solution)/shard_map/all_gather | solution.py:24
  82.6 2.2 %copy-start.1 = (bf16[128,32]{0,1:T(8,128)(2,1)S(1)}, bf16[128,32]{0,1:T(8,128)(2,1)}, u32[]{:S(2)}) copy-start(bf16[128,32]{0,1:T(8,128)(2,1)} %param.8) | copy-start | bytes 24580
  87.1 4.4 %copy-start.3 = (s32[16]{0:T(128)S(1)}, s32[16]{0:T(128)}, u32[]{:S(2)}) copy-start(s32[16]{0:T(128)} %param.14) | copy-start | bytes 196
  87.1 5.4 %copy-start.2 = (s32[1,16]{1,0:T(1,128)S(1)}, s32[1,16]{1,0:T(1,128)}, u32[]{:S(2)}) copy-start(s32[1,16]{1,0:T(1,128)} %param.13) | copy-start | bytes 196
  87.1 42.2 %all-to-all-start = ((f32[4,32,5120]{2,1,0:T(8,128)}), f32[4,32,5120]{2,1,0:T(8,128)S(1)}, u32[]{:S(2)}, u32[]{:S(2)}) async-start(f32[4,32,5120]{2,1,0:T(8,128)} %broadcast_in_dim.38), calls=%async_computation | async-start | bytes 5242880 | tf_op jit(solution)/shard_map/all_to_all | solution.py:43
  90.9 87.8 %all-gather.6.cloned.1.call-start = ((), (), s32[]{:S(2)}) async-start(), calls=%async_computation.3 | async-start | bytes 1056768 | tf_op jit(solution)/shard_map/all_gather | solution.py:78
  132.6 2.6 %copy-start = (bf16[32,5120]{1,0:T(8,128)(2,1)}, bf16[32,5120]{1,0:T(8,128)(2,1)S(1)}, u32[]{:S(2)}) copy-start(bf16[32,5120]{1,0:T(8,128)(2,1)S(1)} %get-tuple-element.6) | copy-start | bytes 983044
  137.6 26.3 %all-to-all-start.1 = ((bf16[128,2,640]{2,1,0:T(2,128)(2,1)}), bf16[128,2,640]{2,1,0:T(2,128)(2,1)S(1)}, u32[]{:S(2)}, u32[]{:S(2)}) async-start(bf16[128,2,640]{2,1,0:T(2,128)(2,1)} %reshape.56), calls=%async_computation.1 | async-start | bytes 655360 | tf_op jit(solution)/shard_map/all_to_all | solution.py:76
Sparse Core Ops, SparseCore 0:
  56.2 26.3 all-gather.3
Sparse Core Ops, SparseCore 1:
  94.4 84.3 all-gather.5
where the time goes:
time: 189 us; the launch traced here: 188 us
  blocking collectives  83.7 us (44%)
  waiting for transfers between devices  55.6 us (29%)
  between operations  16.2 us (9%)
  starting transfers between devices  14.3 us (8%)
  local copies, waits for them, and re-layouts  12 us (6%)
  other arithmetic  3.83 us (2%)
  matrix products  2.8 us (1%)
    all_gather x1, blocking collectives, all_blocks(): blocks = lax.all_gather(blocks, axes[k], axis=0, tiled=True)  47 us
    psum x4, blocking collectives, over_axes(): x = lax.psum(x, axis)  36.6 us
    all_gather x1, waiting for transfers between devices, all_blocks(): blocks = lax.all_gather(blocks, axes[k], axis=0, tiled=True)  26.5 us
    all_to_all x1, waiting for transfers between devices, local(): lax.all_to_all(weight_half, FSDP, split_axis=1, concat_axis=0, tiled=True)  15.3 us
    all_gather x1, waiting for transfers between devices, local(): lax.all_gather(tokens, FSDP, axis=1, tiled=True)  13.2 us
    all_to_all x1, starting transfers between devices, local(): lax.all_to_all(weight_half, FSDP, split_axis=1, concat_axis=0, tiled=True)  10.5 us
    unnamed x11, local copies, waits for them, and re-layouts  4.98 us
    all_to_all x1, starting transfers between devices, from_everyone(): lax.all_to_all(jnp.broadcast_to(x[None], (size, *x.shape)), axis, 0, 0, t...  3.78 us
  transfers between devices with their start and end apart: 4, of which 3 were waited for; matrix products, arithmetic and copies ran while one was open for 5% of the time, Pallas kernels for 0%

commit v1 on v0

--- a/solution.py
+++ b/solution.py
@@ -21,7 +21,8 @@
 def all_blocks(x, axes, order):
     blocks = x[None]
     for k in order:
-        blocks = lax.all_gather(blocks, axes[k], axis=0, tiled=True)
+        stack = jnp.stack([blocks] * lax.axis_size(axes[k]))
+        blocks = jnp.concatenate(lax.all_to_all(stack, axes[k], 0, 0), axis=0)
     current = [lax.axis_size(axes[k]) for k in reversed(order)]
     blocks = blocks.reshape(*current, *x.shape)
     turned = sorted(range(len(order)), key=lambda place: order[len(order) - 1 - place])

time: 189 us -> 150 us (0.79)
  waiting for transfers between devices: 55.6 us -> 25 us
  blocking collectives: 83.7 us -> 76.9 us
    all_gather x1 -> x0, blocking collectives: 47 us -> none  [all_blocks(): blocks = lax.all_gather(blocks, axes[k], axis=0, tiled=True)]
    all_to_all x0 -> x2, blocking collectives: none -> 43.5 us  [all_blocks(): blocks = jnp.concatenate(lax.all_to_all(stack, axes[k], 0, 0), axis=0)]
    all_gather x1 -> x0, waiting for transfers between devices: 26.5 us -> none  [all_blocks(): blocks = lax.all_gather(blocks, axes[k], axis=0, tiled=True)]
    all_gather x1, waiting for transfers between devices: 13.2 us -> 8.97 us  [local(): lax.all_gather(tokens, FSDP, axis=1, tiled=True)]
    psum x4, blocking collectives: 36.6 us -> 33.4 us  [over_axes(): x = lax.psum(x, axis)]
    transpose x1 -> x0, local copies, waits for them, and re-layouts: 2.18 us -> none  [all_blocks(): blocks.transpose(*turned, *range(len(order), blocks.ndim))]
    unnamed x11 -> x10, local copies, waits for them, and re-layouts: 4.98 us -> 4.55 us
  transfers between devices with their start and end apart: 4 -> 3, of which waited for: 3 -> 2; matrix products, arithmetic and copies ran while one was open for 5% -> 6% of each run, Pallas kernels for 0% -> 0%
where the time goes in v1:
time: 150 us; the launch traced here: 149 us
  blocking collectives  76.9 us (51%)
  waiting for transfers between devices  25 us (17%)
  starting transfers between devices  15.5 us (10%)
  between operations  14.8 us (10%)
  local copies, waits for them, and re-layouts  10.3 us (7%)
  other arithmetic  3.94 us (3%)
  matrix products  2.79 us (2%)
    all_to_all x2, blocking collectives, all_blocks(): blocks = jnp.concatenate(lax.all_to_all(stack, axes[k], 0, 0), axis=0)  43.5 us
    psum x4, blocking collectives, over_axes(): x = lax.psum(x, axis)  33.4 us
    all_to_all x1, waiting for transfers between devices, local(): lax.all_to_all(weight_half, FSDP, split_axis=1, concat_axis=0, tiled=True)  15.4 us
    all_to_all x1, starting transfers between devices, local(): lax.all_to_all(weight_half, FSDP, split_axis=1, concat_axis=0, tiled=True)  11.3 us
    all_gather x1, waiting for transfers between devices, local(): lax.all_gather(tokens, FSDP, axis=1, tiled=True)  8.97 us
    unnamed x10, local copies, waits for them, and re-layouts  4.55 us
    all_to_all x1, starting transfers between devices, from_everyone(): lax.all_to_all(jnp.broadcast_to(x[None], (size, *x.shape)), axis, 0, 0, t...  4.15 us
    convert_element_type x1, other arithmetic, local(): weight_half = master_next.astype(jnp.bfloat16)  3.1 us
  transfers between devices with their start and end apart: 3, of which 2 were waited for; matrix products, arithmetic and copies ran while one was open for 6% of the time, Pallas kernels for 0%

profile of v1, /device:TPU:1, one launch (start us, length us, event | category | flops | bytes accessed | tf_op | source)
XLA Modules:
  0.0 149.2 jit_solution(17327392842892053294)
XLA Ops:
  7.2 0.8 stack.6
  8.0 35.5 %all_to_all.34 = bf16[64,1,128,40]{2,3,1,0:T(8,128)(2,1)S(1)} all-to-all(bf16[64,1,128,40]{2,3,1,0:T(8,128)(2,1)S(1)} %stack.6), channel_id=1, replica_groups=mesh['fsdp_0'=8,'fsdp_1'=8,'fsdp_2'=2,'dp'=4] {'fsdp_0','fsdp_1'}, dimensions={0} | all-to-all | bytes 1310720 | tf_op jit(solution)/shard_map/all_to_all | solution.py:25
  43.5 0.1 pad_maximum_fusion
  43.6 8.0 %all_to_all.35 = bf16[2,64,128,40]{2,3,1,0:T(8,128)(2,1)S(1)} all-to-all(bf16[2,64,128,40]{2,3,1,0:T(8,128)(2,1)S(1)} %pad_maximum_fusion), channel_id=1, replica_groups=mesh['fsdp_0'=8,'fsdp_1'=8,'fsdp_2'=2,'dp'=4] {'fsdp_2'}, dimensions={0} | all-to-all | bytes 2621440 | tf_op jit(solution)/shard_map/all_to_all | solution.py:25
  51.6 0.1 copy.19
  51.7 0.6 copy-done.1
  52.3 0.5 convolution_bitcast_fusion
  52.8 1.8 %broadcast_in_dim.34 = f32[4,32,5120]{2,1,0:T(8,128)} broadcast(f32[32,5120]{1,0:T(8,128)S(1)} %convolution_bitcast_fusion), dimensions={1,2} | broadcast | bytes 3276800 | tf_op jit(solution)/shard_map/broadcast_in_dim | solution.py:44
  54.6 4.1 %all-to-all-start.2 = ((f32[4,32,5120]{2,1,0:T(8,128)}), f32[4,32,5120]{2,1,0:T(8,128)S(1)}, u32[]{:S(2)}, u32[]{:S(2)}) async-start(f32[4,32,5120]{2,1,0:T(8,128)} %broadcast_in_dim.34), calls=%async_computation.2 | async-start | bytes 5242880 | tf_op jit(solution)/shard_map/all_to_all | solution.py:44
  58.7 0.7 all-gather.2.cloned.1.call-update
  59.5 0.1 broadcast_in_dim.36
  59.6 0.1 sub.30
  59.6 0.1 broadcast_in_dim.35
  59.7 0.1 sub.28
  60.5 10.4 %psum.28 = s32[16]{0:T(128)S(1)} all-reduce(s32[16]{0:T(128)S(1)} %bitcast.30), channel_id=1, replica_groups=mesh['fsdp_0'=8,'fsdp_1'=8,'fsdp_2'=2,'dp'=4] {'fsdp_0'}, use_global_device_ids=true, to_apply=%region_0.0 | all-reduce | flops 16 | bytes 128 | tf_op jit(solution)/shard_map/psum | solution.py:38
  70.8 8.9 %psum.29 = s32[16]{0:T(128)S(1)} all-reduce(s32[16]{0:T(128)S(1)} %psum.28), channel_id=1, replica_groups=mesh['fsdp_0'=8,'fsdp_1'=8,'fsdp_2'=2,'dp'=4] {'fsdp_1'}, use_global_device_ids=true, to_apply=%region_1.0 | all-reduce | flops 16 | bytes 128 | tf_op jit(solution)/shard_map/psum | solution.py:38
  79.7 6.7 %psum.30 = s32[16]{0:T(128)S(1)} all-reduce(s32[16]{0:T(128)S(1)} %psum.29), channel_id=1, replica_groups=mesh['fsdp_0'=8,'fsdp_1'=8,'fsdp_2'=2,'dp'=4] {'fsdp_2'}, use_global_device_ids=true, to_apply=%region_2.0 | all-reduce | flops 16 | bytes 128 | tf_op jit(solution)/shard_map/psum | solution.py:38
  86.4 7.5 %psum.31 = s32[16]{0:T(128)S(1)} all-reduce(s32[16]{0:T(128)S(1)} %psum.30), channel_id=1, replica_groups=mesh['fsdp_0'=8,'fsdp_1'=8,'fsdp_2'=2,'dp'=4] {'dp'}, use_global_device_ids=true, to_apply=%region_3.0 | all-reduce | flops 16 | bytes 128 | tf_op jit(solution)/shard_map/psum | solution.py:38
  93.9 0.1 broadcast_in_dim.31
  94.0 0.1 broadcast_in_dim.32
  94.1 0.0 all-to-all-done.2
  94.1 0.2 reduce_sum.9
  94.3 3.1 %fusion.4 = (bf16[32,5120]{1,0:T(8,128)(2,1)S(1)}, f32[32,5120]{1,0:T(8,128)}, f32[32,5120]{1,0:T(8,128)}, f32[32,5120]{1,0:T(8,128)}) fusion(f32[32,5120]{1,0:T(8,128)} %param.10, f32[5120]{0:T(1024)S(1)} %sub.30, f32[32,5120]{1,0:T(8,128)S(1)} %reduce_sum.9, f32[32,5120]{1,0:T(8,128)} %param.12, f32[5120]{0:T(1024)S(1)} %sub.28, f32[32,5120]{1,0:T(8,128)} %param.11, ...), kind=kLoop, calls=%fused_computation.14 | loop fusion | flops 2785280 | bytes 4961284 | tf_op jit(solution)/shard_map/convert_element_type | solution.py:75
  97.4 1.9 %all_to_all.26 = bf16[32,128,40]{2,1,0:T(8,128)(2,1)S(1)} reshape(bf16[32,5120]{1,0:T(8,128)(2,1)S(1)} %get-tuple-element.6) | data formatting | bytes 655360 | tf_op jit(solution)/shard_map/all_to_all | solution.py:77
  99.3 0.7 copy.24
  100.0 2.3 %reshape.53 = bf16[128,2,640]{2,1,0:T(2,128)(2,1)} reshape(bf16[128,32,40]{2,1,0:T(8,128)(2,1)S(1)} %bitcast.28) | data formatting | bytes 655360
  102.3 11.3 %all-to-all-start.3 = ((bf16[128,2,640]{2,1,0:T(2,128)(2,1)}), bf16[128,2,640]{2,1,0:T(2,128)(2,1)S(1)}, u32[]{:S(2)}, u32[]{:S(2)}) async-start(bf16[128,2,640]{2,1,0:T(2,128)(2,1)} %reshape.53), calls=%async_computation.3 | async-start | bytes 655360 | tf_op jit(solution)/shard_map/all_to_all | solution.py:77
  113.7 0.5 convert_add_fusion
  114.2 15.4 %all-to-all-done.3 = bf16[128,2,640]{2,1,0:T(2,128)(2,1)S(1)} async-done(((bf16[128,2,640]{2,1,0:T(2,128)(2,1)}), bf16[128,2,640]{2,1,0:T(2,128)(2,1)S(1)}, u32[]{:S(2)}, u32[]{:S(2)}) %all-to-all-start.3) | async-done | bytes 327712 | tf_op jit(solution)/shard_map/all_to_all | solution.py:77
  129.5 1.6 %reshape.54 = bf16[128,32,40]{2,1,0:T(8,128)(2,1)S(1)} reshape(bf16[128,2,640]{2,1,0:T(2,128)(2,1)S(1)} %all-to-all-done.3) | data formatting | bytes 655360
  131.2 9.0 %all-gather.2.cloned.1.call-done = bf16[128,4096]{0,1:T(8,128)(2,1)} async-done(((bf16[128,32]{0,1:T(8,128)(2,1)}), bf16[128,4096]{0,1:T(8,128)(2,1)}) %all-gather.2.cloned.1.call-update) | async-done | bytes 1048592 | tf_op jit(solution)/shard_map/all_gather | solution.py:79
  140.1 2.3 %fusion = bf16[128,40]{0,1:T(8,128)(2,1)} fusion(bf16[4096,40]{1,0:T(8,128)(2,1)S(1)} %bitcast.27, bf16[128,4096]{0,1:T(8,128)(2,1)} %all-gather.2.cloned.1.call-done), kind=kOutput, calls=%fused_computation.3 | convolution fusion | flops 41948160 | bytes 1386496 | tf_op jit(solution)/shard_map/dot_general | solution.py:78
  (10 shorter events, 0.0 us)
Async XLA Ops:
  51.6 0.7 copy-start.1
  54.6 4.9 %copy-start.3 = (s32[16]{0:T(128)S(1)}, s32[16]{0:T(128)}, u32[]{:S(2)}) copy-start(s32[16]{0:T(128)} %param.14) | copy-start | bytes 196
  54.6 5.9 %copy-start.2 = (s32[1,16]{1,0:T(1,128)S(1)}, s32[1,16]{1,0:T(1,128)}, u32[]{:S(2)}) copy-start(s32[1,16]{1,0:T(1,128)} %param.13) | copy-start | bytes 196
  54.6 39.5 %all-to-all-start.2 = ((f32[4,32,5120]{2,1,0:T(8,128)}), f32[4,32,5120]{2,1,0:T(8,128)S(1)}, u32[]{:S(2)}, u32[]{:S(2)}) async-start(f32[4,32,5120]{2,1,0:T(8,128)} %broadcast_in_dim.34), calls=%async_computation.2 | async-start | bytes 5242880 | tf_op jit(solution)/shard_map/all_to_all | solution.py:44
  58.7 81.4 %all-gather.2.cloned.1.call-start = ((), (), s32[]{:S(2)}) async-start(), calls=%async_computation.4 | async-start | bytes 1056768 | tf_op jit(solution)/shard_map/all_gather | solution.py:79
  97.4 2.6 %copy-start = (bf16[32,5120]{1,0:T(8,128)(2,1)}, bf16[32,5120]{1,0:T(8,128)(2,1)S(1)}, u32[]{:S(2)}) copy-start(bf16[32,5120]{1,0:T(8,128)(2,1)S(1)} %get-tuple-element.6) | copy-start | bytes 983044
  102.3 27.2 %all-to-all-start.3 = ((bf16[128,2,640]{2,1,0:T(2,128)(2,1)}), bf16[128,2,640]{2,1,0:T(2,128)(2,1)S(1)}, u32[]{:S(2)}, u32[]{:S(2)}) async-start(bf16[128,2,640]{2,1,0:T(2,128)(2,1)} %reshape.53), calls=%async_computation.3 | async-start | bytes 655360 | tf_op jit(solution)/shard_map/all_to_all | solution.py:77
Sparse Core Ops, SparseCore 0:
  62.6 77.5 all-gather.1
